TPU v7x, 32 devices: a whole 2x2x4 slice. The times are simulated.
32 devices in a mesh: groups: 2 (over x), gx: 8 (over z, y), gy: 2 (over core).
Axes of the slice: x: 2, y: 2, z: 4, core: 2. Of those that a mesh axis runs over, the one named last changes fastest.
Arguments:
- source: float32 [2, 3, 2, 32, 64, 256], P('groups', None, None, 'gx', 'gy'), parts along dimension 0, may hold values from -12 to 12
- permittivity: float32 [6, 32, 64, 256], P('groups', 'gx', 'gy'), parts along dimension 0, may hold values from 1 to 12
- frequency: float32 [1], replicated, may hold values from 0.25 to 0.6
Outputs:
- solution: float32 [2, 3, 2, 32, 64, 256], P('groups', None, None, 'gx', 'gy'), parts along dimension 0
- residual: float32 [2, 3, 2, 32, 64, 256], P('groups', None, None, 'gx', 'gy'), parts along dimension 0
There are 2 independent parts, one for each index of `groups`. A program takes and returns all parts, laid end to end along the dimension named above; an argument that names none is the same for every part. Nothing has to cross between parts.
All inputs are finite; a program needn't handle non-finite values.
Results may differ from a plain program's by a relative error of at most 0.0003.
Values sent between devices are 32-bit elements; how exact they have to be, the bound alone decides.
A program may use at most 64 MiB of HBM per device.

v0:
```python
import jax
import jax.numpy as jnp
from jax import lax
from jax.sharding import PartitionSpec as P

NZ = 256
PML = 8
ITERS = 3
pml_strength = 2.0


def shifted(array, axis, by):
    devices = lax.axis_size(axis)
    pairs = [(i, i + by) for i in range(devices) if 0 <= i + by < devices]
    return lax.ppermute(array, axis, pairs)


def stretch(points, length, frequency):
    inside = jnp.maximum(jnp.maximum(PML - points, points - (length - PML)), 0.0) / PML
    damping = pml_strength * inside**3 / frequency[:, None]
    factor = 1.0 / (1.0 + damping * damping)
    return jnp.stack([factor, -damping * factor], axis=1)


def orient(coefficient, dimension):
    target = [coefficient.shape[0], 2, 1, 1, 1]
    target[dimension] = coefficient.shape[2]
    return coefficient.reshape(target)


def times_coef(values, coefficient):
    real_part = values[:, 0] * coefficient[:, 0] - values[:, 1] * coefficient[:, 1]
    imag_part = values[:, 0] * coefficient[:, 1] + values[:, 1] * coefficient[:, 0]
    return jnp.stack([real_part, imag_part], axis=1)


def curl_forward(extended, front_x, front_y, front_z):
    centre = extended[:, :, :, :-1, :-1]

    def step_x(component):
        return extended[:, component, :, 1:, :-1] - centre[:, component]

    def step_y(component):
        return extended[:, component, :, :-1, 1:] - centre[:, component]

    def step_z(component):
        cells = centre[:, component]
        above = jnp.concatenate([cells[..., 1:], jnp.zeros_like(cells[..., :1])], axis=-1)
        return above - cells

    curl_x = times_coef(step_y(2), front_y) - times_coef(step_z(1), front_z)
    curl_y = times_coef(step_z(0), front_z) - times_coef(step_x(2), front_x)
    curl_z = times_coef(step_x(1), front_x) - times_coef(step_y(0), front_y)
    return jnp.stack([curl_x, curl_y, curl_z], axis=1)


def curl_backward(padded, back_x, back_y, back_z):
    centre = padded[:, :, :, 1:, 1:]

    def step_x(component):
        return centre[:, component] - padded[:, component, :, :-1, 1:]

    def step_y(component):
        return centre[:, component] - padded[:, component, :, 1:, :-1]

    def step_z(component):
        cells = centre[:, component]
        below = jnp.concatenate([jnp.zeros_like(cells[..., :1]), cells[..., :-1]], axis=-1)
        return cells - below

    out_x = times_coef(step_y(2), back_y) - times_coef(step_z(1), back_z)
    out_y = times_coef(step_z(0), back_z) - times_coef(step_x(2), back_x)
    out_z = times_coef(step_x(1), back_x) - times_coef(step_y(0), back_y)
    return jnp.stack([out_x, out_y, out_z], axis=1)


def scaled(values, number):
    real_scale = number[0].reshape(-1, 1, 1, 1, 1)
    imag_scale = number[1].reshape(-1, 1, 1, 1, 1)
    real_part = values[:, :, 0] * real_scale - values[:, :, 1] * imag_scale
    imag_part = values[:, :, 0] * imag_scale + values[:, :, 1] * real_scale
    return jnp.stack([real_part, imag_part], axis=2)


def product(left, right):
    real_part = jnp.sum(
        left[:, :, 0] * right[:, :, 0] + left[:, :, 1] * right[:, :, 1], axis=(1, 2, 3, 4)
    )
    imag_part = jnp.sum(
        left[:, :, 0] * right[:, :, 1] - left[:, :, 1] * right[:, :, 0], axis=(1, 2, 3, 4)
    )
    return jnp.stack([real_part, imag_part])


def complex_times(first, other):
    return jnp.stack(
        [first[0] * other[0] - first[1] * other[1], first[0] * other[1] + first[1] * other[0]]
    )


def complex_ratio(first, other):
    modulus = other[0] * other[0] + other[1] * other[1]
    return (
        jnp.stack(
            [first[0] * other[0] + first[1] * other[1], first[1] * other[0] - first[0] * other[1]]
        )
        / modulus
    )


def grid_points(start, first, count):
    return (start + jnp.arange(first, count, dtype=jnp.int32)).astype(jnp.float32)


def body(source, permittivity, frequency):
    cells_x = source.shape[3]
    cells_y = source.shape[4]
    total_x = cells_x * lax.axis_size("gx")
    total_y = cells_y * lax.axis_size("gy")
    index_x = lax.axis_index("gx")
    index_y = lax.axis_index("gy")
    margin = 0
    front_x = orient(
        stretch(grid_points(index_x * cells_x, -margin, cells_x) + 0.5, total_x, frequency), 2
    )
    front_y = orient(
        stretch(grid_points(index_y * cells_y, -margin, cells_y) + 0.5, total_y, frequency), 3
    )
    back_x = orient(stretch(grid_points(index_x * cells_x, 0, cells_x), total_x, frequency), 2)
    back_y = orient(stretch(grid_points(index_y * cells_y, 0, cells_y), total_y, frequency), 3)
    z_points = grid_points(0, 0, NZ)
    front_z = orient(stretch(z_points + 0.5, NZ, frequency), 4)
    back_z = orient(stretch(z_points, NZ, frequency), 4)
    material = (frequency * frequency).reshape(-1, 1, 1, 1, 1, 1) * permittivity[None, :, None]

    def operate(values):
        above_x = shifted(values[:, :, :, :1], "gx", -1)
        above_y = shifted(values[:, :, :, :, :1], "gy", -1)
        extended = jnp.concatenate([values, above_x], axis=3)
        side_cells = jnp.concatenate([above_y, jnp.zeros_like(above_y[:, :, :, :1])], axis=3)
        extended = jnp.concatenate([extended, side_cells], axis=4)
        rotated = curl_forward(extended, front_x, front_y, front_z)
        below_x = shifted(rotated[:, :, :, -1:], "gx", 1)
        below_y = shifted(rotated[:, :, :, :, -1:], "gy", 1)
        padded = jnp.concatenate([below_x, rotated], axis=3)
        side_cells = jnp.concatenate([jnp.zeros_like(below_y[:, :, :, :1]), below_y], axis=3)
        padded = jnp.concatenate([side_cells, padded], axis=4)
        applied = curl_backward(padded, back_x, back_y, back_z)
        return applied - material * values

    solution = jnp.zeros_like(source)
    residual = source
    direction = source
    shadow_dot = lax.psum(product(source, residual), ("gx", "gy"))
    for iteration in range(ITERS):
        applied = operate(direction)
        step_size = complex_ratio(shadow_dot, lax.psum(product(source, applied), ("gx", "gy")))
        middle = residual - scaled(applied, step_size)
        second = operate(middle)
        sums_triple = lax.psum(
            (product(second, middle), product(second, second), product(source, second)),
            ("gx", "gy"),
        )
        weight = complex_ratio(sums_triple[0], sums_triple[1])
        solution = solution + scaled(direction, step_size) + scaled(middle, weight)
        residual = middle - scaled(second, weight)
        if iteration + 1 < ITERS:
            shadow_next = -complex_times(weight, sums_triple[2])
            momentum = complex_times(
                complex_ratio(shadow_next, shadow_dot), complex_ratio(step_size, weight)
            )
            direction = residual + scaled(direction - scaled(applied, weight), momentum)
            shadow_dot = shadow_next
    return (solution, residual)


def solution(mesh):
    placed = (P("groups", None, None, "gx", "gy", None), P("groups", "gx", "gy", None), P())
    return jax.shard_map(
        body,
        mesh=mesh,
        in_specs=placed,
        out_specs=(
            P("groups", None, None, "gx", "gy", None),
            P("groups", None, None, "gx", "gy", None),
        ),
        check_vma=False,
    )
```

profile of v0, /device:TPU:0, one launch (start us, length us, event | category | flops | bytes accessed | tf_op | source)
XLA Modules:
  0.0 469.3 jit_solution(13969787863053648633)
XLA Ops:
  7.5 6.7 %collective-permute-done = f32[1,3,2,1,32,256]{5,4,3,2,1,0:T(8,128)S(1)} collective-permute-done((f32[1,3,2,1,32,256]{5,4,3,2,1,0:T(8,128)S(1)}, f32[1,3,2,1,32,256]{5,4,3,2,1,0:T(8,128)S(1)}, u32[]{:S(2)}, u32[]{:S(2)}) %collective-permute-start) | collective-permute-done | bytes 196640 | tf_op jit(solution)/shard_map/ppermute | solution.py:15
  17.5 5.0 %collective-permute-start.3 = (f32[1,3,2,1,32,256]{5,4,3,2,1,0:T(8,128)S(1)}, f32[1,3,2,1,32,256]{5,4,3,2,1,0:T(8,128)S(1)}, u32[]{:S(2)}, u32[]{:S(2)}) collective-permute-start(f32[1,3,2,1,32,256]{5,4,3,2,1,0:T(8,128)S(1)} %pad_maximum_fusion.33), channel_id=1, source_target_pairs={{0,2},{2,4},{4,6},{6,8},{8,10},{10,12},{12,14},{1,3},{3,5},{5,7},{... | collective-permute-start | bytes 589832 | tf_op jit(solution)/shard_map/ppermute | solution.py:15
  22.5 3.6 collective-permute-done.3
  31.1 31.3 %all-reduce.39 = (f32[2,1]{1,0:T(2,128)S(1)}, f32[2,1]{1,0:T(2,128)S(1)}) all-reduce(f32[2,1]{1,0:T(2,128)S(1)} %pad_maximum_fusion.41, f32[2,1]{1,0:T(2,128)S(1)} %pad_maximum_fusion.42), channel_id=1, replica_groups=mesh['groups'=2,'gx'=8,'gy'=2] {'gx','gy'}, use_global_device_ids=true, to_apply=%region_2.0 | all-reduce | flops 4 | bytes 32 | tf_op jit(solution)/shard_map/psum | solution.py:154
  77.4 3.2 collective-permute-done.4
  94.9 29.5 %all-reduce.38 = (f32[2,1]{1,0:T(2,128)S(1)}, f32[2,1]{1,0:T(2,128)S(1)}, f32[2,1]{1,0:T(2,128)S(1)}) all-reduce(f32[2,1]{1,0:T(2,128)S(1)} %pad_maximum_fusion.43, f32[2,1]{1,0:T(2,128)S(1)} %pad_maximum_fusion.44, f32[2,1]{1,0:T(2,128)S(1)} %pad_maximum_fusion.45), channel_id=1, replica_groups=mesh['groups'=2,'gx'=8,'gy'=2] {'gx','gy'}, use_global_device_ids=true, to_apply=%region_8.0 | all-reduce | flops 6 | bytes 48 | tf_op jit(solution)/shard_map/psum | solution.py:160
  141.5 2.5 multiply_subtract_fusion.11
  168.3 4.2 collective-permute-done.8
  183.4 30.3 %psum.89 = f32[2,1]{1,0:T(2,128)S(1)} all-reduce(f32[2,1]{1,0:T(2,128)S(1)} %pad_maximum_fusion.46), channel_id=1, replica_groups=mesh['groups'=2,'gx'=8,'gy'=2] {'gx','gy'}, use_global_device_ids=true, to_apply=%region_17.0 | all-reduce | flops 2 | bytes 16 | tf_op jit(solution)/shard_map/psum | solution.py:157
  222.7 2.5 multiply_subtract_fusion.8
  230.0 3.4 collective-permute-done.12
  251.3 30.6 %all-reduce.37 = (f32[2,1]{1,0:T(2,128)}, f32[2,1]{1,0:T(2,128)}, f32[2,1]{1,0:T(2,128)}) all-reduce(f32[2,1]{1,0:T(2,128)} %pad_maximum_fusion.47, f32[2,1]{1,0:T(2,128)} %pad_maximum_fusion.48, f32[2,1]{1,0:T(2,128)} %pad_maximum_fusion.49), channel_id=1, replica_groups=mesh['groups'=2,'gx'=8,'gy'=2] {'gx','gy'}, use_global_device_ids=true, to_apply=%region_20.0 | all-reduce | flops 6 | bytes 48 | tf_op jit(solution)/shard_map/psum | solution.py:160
  300.1 2.5 multiply_subtract_fusion.5
  327.7 3.7 collective-permute-done.16
  342.3 3.0 add_reduce_fusion.2
  347.1 2.3 multiply_subtract_fusion.13
  349.4 30.0 %psum.93 = f32[2,1]{1,0:T(2,128)S(1)} all-reduce(f32[2,1]{1,0:T(2,128)} %pad_maximum_fusion.50), channel_id=1, replica_groups=mesh['groups'=2,'gx'=8,'gy'=2] {'gx','gy'}, use_global_device_ids=true, to_apply=%region_29.0 | all-reduce | flops 2 | bytes 16 | tf_op jit(solution)/shard_map/psum | solution.py:157
  388.2 2.5 multiply_subtract_fusion.2
  390.7 2.3 maximum_subtract_fusion.11
  395.6 2.3 multiply_subtract_fusion.9
  397.9 5.9 %collective-permute-done.20 = f32[1,3,2,1,32,256]{5,4,3,2,1,0:T(8,128)S(1)} collective-permute-done((f32[1,3,2,1,32,256]{5,4,3,2,1,0:T(8,128)S(1)}, f32[1,3,2,1,32,256]{5,4,3,2,1,0:T(8,128)S(1)}, u32[]{:S(2)}, u32[]{:S(2)}) %collective-permute-start.20) | collective-permute-done | bytes 196640 | tf_op jit(solution)/shard_map/ppermute | solution.py:15
  420.7 2.2 multiply_subtract_fusion.3
  422.9 29.5 %all-reduce.36 = (f32[2,1]{1,0:T(2,128)S(1)}, f32[2,1]{1,0:T(2,128)S(1)}) all-reduce(f32[2,1]{1,0:T(2,128)S(1)} %pad_maximum_fusion.51, f32[2,1]{1,0:T(2,128)S(1)} %pad_maximum_fusion.52), channel_id=1, replica_groups=mesh['groups'=2,'gx'=8,'gy'=2] {'gx','gy'}, use_global_device_ids=true, to_apply=%region_32.0 | all-reduce | flops 4 | bytes 32 | tf_op jit(solution)/shard_map/psum | solution.py:160
  461.4 2.6 multiply_subtract_fusion
  (463 shorter events, 127.9 us)
Async XLA Ops:
  1.6 12.5 %collective-permute-start.1 = (f32[1,3,2,4,1,256]{5,4,3,2,1,0:T(1,128)S(1)}, f32[1,3,2,4,1,256]{5,4,3,2,1,0:T(1,128)S(1)}, u32[]{:S(2)}, u32[]{:S(2)}) collective-permute-start(f32[1,3,2,4,1,256]{5,4,3,2,1,0:T(1,128)S(1)} %slice.702), channel_id=1, source_target_pairs={{1,0},{3,2},{5,4},{7,6},{9,8},{11,10},{13,12},{15,14},{17,16},{19,... | collective-permute-start | bytes 73736 | tf_op jit(solution)/shard_map/ppermute | solution.py:15
  3.9 10.2 %collective-permute-start = (f32[1,3,2,1,32,256]{5,4,3,2,1,0:T(8,128)S(1)}, f32[1,3,2,1,32,256]{5,4,3,2,1,0:T(8,128)S(1)}, u32[]{:S(2)}, u32[]{:S(2)}) collective-permute-start(f32[1,3,2,1,32,256]{5,4,3,2,1,0:T(8,128)S(1)} %slice.695), channel_id=1, source_target_pairs={{2,0},{4,2},{6,4},{8,6},{10,8},{12,10},{14,12},{3,1},{5,3},{7,5},{... | collective-permute-start | bytes 589832 | tf_op jit(solution)/shard_map/ppermute | solution.py:15
  15.4 7.2 %collective-permute-start.2 = (f32[1,3,2,4,1,256]{5,4,3,2,1,0:T(1,128)S(1)}, f32[1,3,2,4,1,256]{5,4,3,2,1,0:T(1,128)S(1)}, u32[]{:S(2)}, u32[]{:S(2)}) collective-permute-start(f32[1,3,2,4,1,256]{5,4,3,2,1,0:T(1,128)S(1)} %pad_maximum_fusion.40), channel_id=1, source_target_pairs={{0,1},{2,3},{4,5},{6,7},{8,9},{10,11},{12,13},{14,15},{16,17},{18,... | collective-permute-start | bytes 73736 | tf_op jit(solution)/shard_map/ppermute | solution.py:15
  17.5 8.7 %collective-permute-start.3 = (f32[1,3,2,1,32,256]{5,4,3,2,1,0:T(8,128)S(1)}, f32[1,3,2,1,32,256]{5,4,3,2,1,0:T(8,128)S(1)}, u32[]{:S(2)}, u32[]{:S(2)}) collective-permute-start(f32[1,3,2,1,32,256]{5,4,3,2,1,0:T(8,128)S(1)} %pad_maximum_fusion.33), channel_id=1, source_target_pairs={{0,2},{2,4},{4,6},{6,8},{8,10},{10,12},{12,14},{1,3},{3,5},{5,7},{... | collective-permute-start | bytes 589832 | tf_op jit(solution)/shard_map/ppermute | solution.py:15
  73.0 7.6 %collective-permute-start.4 = (f32[1,3,2,1,32,256]{5,4,3,2,1,0:T(8,128)S(1)}, f32[1,3,2,1,32,256]{5,4,3,2,1,0:T(8,128)S(1)}, u32[]{:S(2)}, u32[]{:S(2)}) collective-permute-start(f32[1,3,2,1,32,256]{5,4,3,2,1,0:T(8,128)S(1)} %slice.2127), channel_id=1, source_target_pairs={{2,0},{4,2},{6,4},{8,6},{10,8},{12,10},{14,12},{3,1},{5,3},{7,5},{... | collective-permute-start | bytes 589832 | tf_op jit(solution)/shard_map/ppermute | solution.py:15
  74.3 3.1 collective-permute-start.5
  81.7 5.9 %collective-permute-start.7 = (f32[1,3,2,1,32,256]{5,4,3,2,1,0:T(8,128)S(1)}, f32[1,3,2,1,32,256]{5,4,3,2,1,0:T(8,128)S(1)}, u32[]{:S(2)}, u32[]{:S(2)}) collective-permute-start(f32[1,3,2,1,32,256]{5,4,3,2,1,0:T(8,128)S(1)} %pad_maximum_fusion.31), channel_id=1, source_target_pairs={{0,2},{2,4},{4,6},{6,8},{8,10},{10,12},{12,14},{1,3},{3,5},{5,7},{... | collective-permute-start | bytes 589832 | tf_op jit(solution)/shard_map/ppermute | solution.py:15
  83.2 4.4 collective-permute-start.6
  163.9 8.6 %collective-permute-start.8 = (f32[1,3,2,1,32,256]{5,4,3,2,1,0:T(8,128)S(1)}, f32[1,3,2,1,32,256]{5,4,3,2,1,0:T(8,128)S(1)}, u32[]{:S(2)}, u32[]{:S(2)}) collective-permute-start(f32[1,3,2,1,32,256]{5,4,3,2,1,0:T(8,128)S(1)} %slice.2170), channel_id=1, source_target_pairs={{2,0},{4,2},{6,4},{8,6},{10,8},{12,10},{14,12},{3,1},{5,3},{7,5},{... | collective-permute-start | bytes 589832 | tf_op jit(solution)/shard_map/ppermute | solution.py:15
  165.2 3.1 collective-permute-start.9
  173.6 4.9 %collective-permute-start.11 = (f32[1,3,2,1,32,256]{5,4,3,2,1,0:T(8,128)S(1)}, f32[1,3,2,1,32,256]{5,4,3,2,1,0:T(8,128)S(1)}, u32[]{:S(2)}, u32[]{:S(2)}) collective-permute-start(f32[1,3,2,1,32,256]{5,4,3,2,1,0:T(8,128)S(1)} %pad_maximum_fusion.29), channel_id=1, source_target_pairs={{0,2},{2,4},{4,6},{6,8},{8,10},{10,12},{12,14},{1,3},{3,5},{5,7},{... | collective-permute-start | bytes 589832 | tf_op jit(solution)/shard_map/ppermute | solution.py:15
  175.1 2.1 collective-permute-start.10
  225.6 7.8 %collective-permute-start.12 = (f32[1,3,2,1,32,256]{5,4,3,2,1,0:T(8,128)S(1)}, f32[1,3,2,1,32,256]{5,4,3,2,1,0:T(8,128)S(1)}, u32[]{:S(2)}, u32[]{:S(2)}) collective-permute-start(f32[1,3,2,1,32,256]{5,4,3,2,1,0:T(8,128)S(1)} %slice.2211), channel_id=1, source_target_pairs={{2,0},{4,2},{6,4},{8,6},{10,8},{12,10},{14,12},{3,1},{5,3},{7,5},{... | collective-permute-start | bytes 589832 | tf_op jit(solution)/shard_map/ppermute | solution.py:15
  226.9 3.1 collective-permute-start.13
  235.0 5.6 %collective-permute-start.15 = (f32[1,3,2,1,32,256]{5,4,3,2,1,0:T(8,128)S(1)}, f32[1,3,2,1,32,256]{5,4,3,2,1,0:T(8,128)S(1)}, u32[]{:S(2)}, u32[]{:S(2)}) collective-permute-start(f32[1,3,2,1,32,256]{5,4,3,2,1,0:T(8,128)S(1)} %pad_maximum_fusion.27), channel_id=1, source_target_pairs={{0,2},{2,4},{4,6},{6,8},{8,10},{10,12},{12,14},{1,3},{3,5},{5,7},{... | collective-permute-start | bytes 589832 | tf_op jit(solution)/shard_map/ppermute | solution.py:15
  236.5 4.0 collective-permute-start.14
  323.3 8.1 %collective-permute-start.16 = (f32[1,3,2,1,32,256]{5,4,3,2,1,0:T(8,128)S(1)}, f32[1,3,2,1,32,256]{5,4,3,2,1,0:T(8,128)S(1)}, u32[]{:S(2)}, u32[]{:S(2)}) collective-permute-start(f32[1,3,2,1,32,256]{5,4,3,2,1,0:T(8,128)S(1)} %slice.2254), channel_id=1, source_target_pairs={{2,0},{4,2},{6,4},{8,6},{10,8},{12,10},{14,12},{3,1},{5,3},{7,5},{... | collective-permute-start | bytes 589832 | tf_op jit(solution)/shard_map/ppermute | solution.py:15
  324.6 3.1 collective-permute-start.17
  333.0 5.3 %collective-permute-start.19 = (f32[1,3,2,1,32,256]{5,4,3,2,1,0:T(8,128)S(1)}, f32[1,3,2,1,32,256]{5,4,3,2,1,0:T(8,128)S(1)}, u32[]{:S(2)}, u32[]{:S(2)}) collective-permute-start(f32[1,3,2,1,32,256]{5,4,3,2,1,0:T(8,128)S(1)} %pad_maximum_fusion.25), channel_id=1, source_target_pairs={{0,2},{2,4},{4,6},{6,8},{8,10},{10,12},{12,14},{1,3},{3,5},{5,7},{... | collective-permute-start | bytes 589832 | tf_op jit(solution)/shard_map/ppermute | solution.py:15
  334.6 2.1 collective-permute-start.18
  393.0 5.0 %collective-permute-start.21 = (f32[1,3,2,4,1,256]{5,4,3,2,1,0:T(1,128)S(1)}, f32[1,3,2,4,1,256]{5,4,3,2,1,0:T(1,128)S(1)}, u32[]{:S(2)}, u32[]{:S(2)}) collective-permute-start(f32[1,3,2,4,1,256]{5,4,3,2,1,0:T(1,128)S(1)} %slice.2299), channel_id=1, source_target_pairs={{1,0},{3,2},{5,4},{7,6},{9,8},{11,10},{13,12},{15,14},{17,16},{19,... | collective-permute-start | bytes 73736 | tf_op jit(solution)/shard_map/ppermute | solution.py:15
  394.3 9.5 %collective-permute-start.20 = (f32[1,3,2,1,32,256]{5,4,3,2,1,0:T(8,128)S(1)}, f32[1,3,2,1,32,256]{5,4,3,2,1,0:T(8,128)S(1)}, u32[]{:S(2)}, u32[]{:S(2)}) collective-permute-start(f32[1,3,2,1,32,256]{5,4,3,2,1,0:T(8,128)S(1)} %slice.2295), channel_id=1, source_target_pairs={{2,0},{4,2},{6,4},{8,6},{10,8},{12,10},{14,12},{3,1},{5,3},{7,5},{... | collective-permute-start | bytes 589832 | tf_op jit(solution)/shard_map/ppermute | solution.py:15
  405.4 6.1 %collective-permute-start.22 = (f32[1,3,2,4,1,256]{5,4,3,2,1,0:T(1,128)S(1)}, f32[1,3,2,4,1,256]{5,4,3,2,1,0:T(1,128)S(1)}, u32[]{:S(2)}, u32[]{:S(2)}) collective-permute-start(f32[1,3,2,4,1,256]{5,4,3,2,1,0:T(1,128)S(1)} %pad_maximum_fusion.35), channel_id=1, source_target_pairs={{0,1},{2,3},{4,5},{6,7},{8,9},{10,11},{12,13},{14,15},{16,17},{18,... | collective-permute-start | bytes 73736 | tf_op jit(solution)/shard_map/ppermute | solution.py:15
  407.5 5.3 %collective-permute-start.23 = (f32[1,3,2,1,32,256]{5,4,3,2,1,0:T(8,128)S(1)}, f32[1,3,2,1,32,256]{5,4,3,2,1,0:T(8,128)S(1)}, u32[]{:S(2)}, u32[]{:S(2)}) collective-permute-start(f32[1,3,2,1,32,256]{5,4,3,2,1,0:T(8,128)S(1)} %pad_maximum_fusion.23), channel_id=1, source_target_pairs={{0,2},{2,4},{4,6},{6,8},{8,10},{10,12},{12,14},{1,3},{3,5},{5,7},{... | collective-permute-start | bytes 589832 | tf_op jit(solution)/shard_map/ppermute | solution.py:15
  (86 other events, 1988.6 us)
where the time goes:
time: 472 us; the launch traced here: 469 us
  blocking collectives  181 us (38%)
  between operations  99.9 us (21%)
  other arithmetic  74.5 us (16%)
  waiting for transfers between devices  43.6 us (9%)
  starting transfers between devices  38.4 us (8%)
  local copies, waits for them, and re-layouts  31.8 us (7%)
    psum x3, blocking collectives, body(): lax.psum((product(second, middle), product(second, second), product(sourc...  89.6 us
    psum x2, blocking collectives, body(): lax.psum(product(source, applied), ('gx', 'gy'))  60.3 us
    ppermute x24, waiting for transfers between devices, shifted(): return lax.ppermute(array, axis, pairs)  43.6 us
    ppermute x24, starting transfers between devices, shifted(): return lax.ppermute(array, axis, pairs)  38.4 us
    psum x1, blocking collectives, body(): shadow_dot = lax.psum(product(source, residual), ('gx', 'gy'))  31.3 us
    sub x15, other arithmetic, scaled(): real_part = values[:, :, 0] * real_scale - values[:, :, 1] * imag_scale  27.3 us
    another operation x12, other arithmetic, product(): return jnp.stack([real_part, imag_part])  17.5 us
    unnamed x173, local copies, waits for them, and re-layouts  12.9 us
  transfers between devices with their start and end apart: 24, of which 17 were waited for; matrix products, arithmetic and copies ran while one was open for 2% of the time, Pallas kernels for 0%

commit v1 on v0

--- a/solution.py
+++ b/solution.py
@@ -151,7 +151,8 @@
     solution = jnp.zeros_like(source)
     residual = source
     direction = source
-    shadow_dot = lax.psum(product(source, residual), ("gx", "gy"))
+    half = lax.psum(product(source, residual), "gx")
+    shadow_dot = lax.psum(half, "gy")
     for iteration in range(ITERS):
         applied = operate(direction)
         step_size = complex_ratio(shadow_dot, lax.psum(product(source, applied), ("gx", "gy")))

time: 472 us -> 494 us (1.047)
  blocking collectives: 181 us -> 201 us
    psum x2 -> x3, blocking collectives: 60.3 us -> 91.6 us  [body(): lax.psum(product(source, applied), ('gx', 'gy'))]
    psum x1 -> x2, blocking collectives: 31.3 us -> 19.6 us  [the longest x1 17.1 us: body(): half = lax.psum(product(source, residual), 'gx')]
  transfers between devices with their start and end apart: 24 -> 24, of which waited for: 17 -> 17; matrix products, arithmetic and copies ran while one was open for 2% -> 1% of each run, Pallas kernels for 0% -> 0%
where the time goes in v1:
time: 494 us; the launch traced here: 491 us
  blocking collectives  201 us (41%)
  between operations  98 us (20%)
  other arithmetic  74.2 us (15%)
  waiting for transfers between devices  45.3 us (9%)
  starting transfers between devices  41 us (8%)
  local copies, waits for them, and re-layouts  31.6 us (6%)
    psum x3, blocking collectives, body(): lax.psum(product(source, applied), ('gx', 'gy'))  91.6 us
    psum x3, blocking collectives, body(): lax.psum((product(second, middle), product(second, second), product(sourc...  89.6 us
    ppermute x24, waiting for transfers between devices, shifted(): return lax.ppermute(array, axis, pairs)  45.3 us
    ppermute x24, starting transfers between devices, shifted(): return lax.ppermute(array, axis, pairs)  41 us
    sub x15, other arithmetic, scaled(): real_part = values[:, :, 0] * real_scale - values[:, :, 1] * imag_scale  27 us
    another operation x12, other arithmetic, product(): return jnp.stack([real_part, imag_part])  17.5 us
    psum x1, blocking collectives, body(): half = lax.psum(product(source, residual), 'gx')  17.1 us
    unnamed x173, local copies, waits for them, and re-layouts  13 us
  transfers between devices with their start and end apart: 24, of which 17 were waited for; matrix products, arithmetic and copies ran while one was open for 1% of the time, Pallas kernels for 0%

profile of v1, /device:TPU:0, one launch (start us, length us, event | category | flops | bytes accessed | tf_op | source)
XLA Modules:
  0.0 490.9 jit_solution(12805036179765152023)
XLA Ops:
  7.5 6.7 %collective-permute-done = f32[1,3,2,1,32,256]{5,4,3,2,1,0:T(8,128)S(1)} collective-permute-done((f32[1,3,2,1,32,256]{5,4,3,2,1,0:T(8,128)S(1)}, f32[1,3,2,1,32,256]{5,4,3,2,1,0:T(8,128)S(1)}, u32[]{:S(2)}, u32[]{:S(2)}) %collective-permute-start) | collective-permute-done | bytes 196640 | tf_op jit(solution)/shard_map/ppermute | solution.py:15
  17.5 5.0 %collective-permute-start.3 = (f32[1,3,2,1,32,256]{5,4,3,2,1,0:T(8,128)S(1)}, f32[1,3,2,1,32,256]{5,4,3,2,1,0:T(8,128)S(1)}, u32[]{:S(2)}, u32[]{:S(2)}) collective-permute-start(f32[1,3,2,1,32,256]{5,4,3,2,1,0:T(8,128)S(1)} %pad_maximum_fusion.33), channel_id=1, source_target_pairs={{0,2},{2,4},{4,6},{6,8},{8,10},{10,12},{12,14},{1,3},{3,5},{5,7},{... | collective-permute-start | bytes 589832 | tf_op jit(solution)/shard_map/ppermute | solution.py:15
  22.5 3.6 collective-permute-done.3
  29.8 31.3 %psum.93 = f32[2,1]{1,0:T(2,128)S(1)} all-reduce(f32[2,1]{1,0:T(2,128)S(1)} %pad_maximum_fusion.42), channel_id=1, replica_groups=mesh['groups'=2,'gx'=8,'gy'=2] {'gx','gy'}, use_global_device_ids=true, to_apply=%region_6.0 | all-reduce | flops 2 | bytes 16 | tf_op jit(solution)/shard_map/psum | solution.py:158
  64.1 17.1 %psum.91 = f32[2,1]{1,0:T(2,128)S(1)} all-reduce(f32[2,1]{1,0:T(2,128)S(1)} %pad_maximum_fusion.41), channel_id=1, replica_groups=mesh['groups'=2,'gx'=8,'gy'=2] {'gx'}, use_global_device_ids=true, to_apply=%region_2.0 | all-reduce | flops 2 | bytes 16 | tf_op jit(solution)/shard_map/psum | solution.py:154
  82.6 2.5 psum.92
  97.3 4.7 collective-permute-done.4
  103.1 4.5 collective-permute-start.7
  118.9 29.5 %all-reduce.38 = (f32[2,1]{1,0:T(2,128)S(1)}, f32[2,1]{1,0:T(2,128)S(1)}, f32[2,1]{1,0:T(2,128)S(1)}) all-reduce(f32[2,1]{1,0:T(2,128)S(1)} %pad_maximum_fusion.43, f32[2,1]{1,0:T(2,128)S(1)} %pad_maximum_fusion.44, f32[2,1]{1,0:T(2,128)S(1)} %pad_maximum_fusion.45), channel_id=1, replica_groups=mesh['groups'=2,'gx'=8,'gy'=2] {'gx','gy'}, use_global_device_ids=true, to_apply=%region_9.0 | all-reduce | flops 6 | bytes 48 | tf_op jit(solution)/shard_map/psum | solution.py:161
  164.4 2.4 multiply_subtract_fusion.11
  190.3 4.2 collective-permute-done.8
  205.3 30.3 %psum.97 = f32[2,1]{1,0:T(2,128)S(1)} all-reduce(f32[2,1]{1,0:T(2,128)S(1)} %pad_maximum_fusion.46), channel_id=1, replica_groups=mesh['groups'=2,'gx'=8,'gy'=2] {'gx','gy'}, use_global_device_ids=true, to_apply=%region_18.0 | all-reduce | flops 2 | bytes 16 | tf_op jit(solution)/shard_map/psum | solution.py:158
  244.2 2.5 multiply_subtract_fusion.8
  251.5 3.4 collective-permute-done.12
  272.9 30.6 %all-reduce.37 = (f32[2,1]{1,0:T(2,128)}, f32[2,1]{1,0:T(2,128)}, f32[2,1]{1,0:T(2,128)}) all-reduce(f32[2,1]{1,0:T(2,128)} %pad_maximum_fusion.47, f32[2,1]{1,0:T(2,128)} %pad_maximum_fusion.48, f32[2,1]{1,0:T(2,128)} %pad_maximum_fusion.49), channel_id=1, replica_groups=mesh['groups'=2,'gx'=8,'gy'=2] {'gx','gy'}, use_global_device_ids=true, to_apply=%region_21.0 | all-reduce | flops 6 | bytes 48 | tf_op jit(solution)/shard_map/psum | solution.py:161
  321.9 2.5 multiply_subtract_fusion.5
  349.4 3.7 collective-permute-done.16
  364.1 3.0 add_reduce_fusion.2
  371.0 30.0 %psum.101 = f32[2,1]{1,0:T(2,128)S(1)} all-reduce(f32[2,1]{1,0:T(2,128)} %pad_maximum_fusion.50), channel_id=1, replica_groups=mesh['groups'=2,'gx'=8,'gy'=2] {'gx','gy'}, use_global_device_ids=true, to_apply=%region_30.0 | all-reduce | flops 2 | bytes 16 | tf_op jit(solution)/shard_map/psum | solution.py:158
  409.5 2.5 multiply_subtract_fusion.2
  419.3 5.9 %collective-permute-done.20 = f32[1,3,2,1,32,256]{5,4,3,2,1,0:T(8,128)S(1)} collective-permute-done((f32[1,3,2,1,32,256]{5,4,3,2,1,0:T(8,128)S(1)}, f32[1,3,2,1,32,256]{5,4,3,2,1,0:T(8,128)S(1)}, u32[]{:S(2)}, u32[]{:S(2)}) %collective-permute-start.20) | collective-permute-done | bytes 196640 | tf_op jit(solution)/shard_map/ppermute | solution.py:15
  442.4 2.3 multiply_subtract_fusion.3
  444.7 29.5 %all-reduce.36 = (f32[2,1]{1,0:T(2,128)S(1)}, f32[2,1]{1,0:T(2,128)S(1)}) all-reduce(f32[2,1]{1,0:T(2,128)S(1)} %pad_maximum_fusion.51, f32[2,1]{1,0:T(2,128)S(1)} %pad_maximum_fusion.52), channel_id=1, replica_groups=mesh['groups'=2,'gx'=8,'gy'=2] {'gx','gy'}, use_global_device_ids=true, to_apply=%region_33.0 | all-reduce | flops 4 | bytes 32 | tf_op jit(solution)/shard_map/psum | solution.py:161
  483.1 2.6 multiply_subtract_fusion
  (465 shorter events, 132.5 us)
Async XLA Ops:
  1.6 12.5 %collective-permute-start.1 = (f32[1,3,2,4,1,256]{5,4,3,2,1,0:T(1,128)S(1)}, f32[1,3,2,4,1,256]{5,4,3,2,1,0:T(1,128)S(1)}, u32[]{:S(2)}, u32[]{:S(2)}) collective-permute-start(f32[1,3,2,4,1,256]{5,4,3,2,1,0:T(1,128)S(1)} %slice.702), channel_id=1, source_target_pairs={{1,0},{3,2},{5,4},{7,6},{9,8},{11,10},{13,12},{15,14},{17,16},{19,... | collective-permute-start | bytes 73736 | tf_op jit(solution)/shard_map/ppermute | solution.py:15
  3.9 10.2 %collective-permute-start = (f32[1,3,2,1,32,256]{5,4,3,2,1,0:T(8,128)S(1)}, f32[1,3,2,1,32,256]{5,4,3,2,1,0:T(8,128)S(1)}, u32[]{:S(2)}, u32[]{:S(2)}) collective-permute-start(f32[1,3,2,1,32,256]{5,4,3,2,1,0:T(8,128)S(1)} %slice.695), channel_id=1, source_target_pairs={{2,0},{4,2},{6,4},{8,6},{10,8},{12,10},{14,12},{3,1},{5,3},{7,5},{... | collective-permute-start | bytes 589832 | tf_op jit(solution)/shard_map/ppermute | solution.py:15
  15.4 7.2 %collective-permute-start.2 = (f32[1,3,2,4,1,256]{5,4,3,2,1,0:T(1,128)S(1)}, f32[1,3,2,4,1,256]{5,4,3,2,1,0:T(1,128)S(1)}, u32[]{:S(2)}, u32[]{:S(2)}) collective-permute-start(f32[1,3,2,4,1,256]{5,4,3,2,1,0:T(1,128)S(1)} %pad_maximum_fusion.40), channel_id=1, source_target_pairs={{0,1},{2,3},{4,5},{6,7},{8,9},{10,11},{12,13},{14,15},{16,17},{18,... | collective-permute-start | bytes 73736 | tf_op jit(solution)/shard_map/ppermute | solution.py:15
  17.5 8.7 %collective-permute-start.3 = (f32[1,3,2,1,32,256]{5,4,3,2,1,0:T(8,128)S(1)}, f32[1,3,2,1,32,256]{5,4,3,2,1,0:T(8,128)S(1)}, u32[]{:S(2)}, u32[]{:S(2)}) collective-permute-start(f32[1,3,2,1,32,256]{5,4,3,2,1,0:T(8,128)S(1)} %pad_maximum_fusion.33), channel_id=1, source_target_pairs={{0,2},{2,4},{4,6},{6,8},{8,10},{10,12},{12,14},{1,3},{3,5},{5,7},{... | collective-permute-start | bytes 589832 | tf_op jit(solution)/shard_map/ppermute | solution.py:15
  92.9 9.1 %collective-permute-start.4 = (f32[1,3,2,1,32,256]{5,4,3,2,1,0:T(8,128)S(1)}, f32[1,3,2,1,32,256]{5,4,3,2,1,0:T(8,128)S(1)}, u32[]{:S(2)}, u32[]{:S(2)}) collective-permute-start(f32[1,3,2,1,32,256]{5,4,3,2,1,0:T(8,128)S(1)} %slice.2127), channel_id=1, source_target_pairs={{2,0},{4,2},{6,4},{8,6},{10,8},{12,10},{14,12},{3,1},{5,3},{7,5},{... | collective-permute-start | bytes 589832 | tf_op jit(solution)/shard_map/ppermute | solution.py:15
  94.2 3.1 collective-permute-start.5
  103.1 8.4 %collective-permute-start.7 = (f32[1,3,2,1,32,256]{5,4,3,2,1,0:T(8,128)S(1)}, f32[1,3,2,1,32,256]{5,4,3,2,1,0:T(8,128)S(1)}, u32[]{:S(2)}, u32[]{:S(2)}) collective-permute-start(f32[1,3,2,1,32,256]{5,4,3,2,1,0:T(8,128)S(1)} %pad_maximum_fusion.31), channel_id=1, source_target_pairs={{0,2},{2,4},{4,6},{6,8},{8,10},{10,12},{12,14},{1,3},{3,5},{5,7},{... | collective-permute-start | bytes 589832 | tf_op jit(solution)/shard_map/ppermute | solution.py:15
  107.7 3.8 collective-permute-start.6
  185.9 8.6 %collective-permute-start.8 = (f32[1,3,2,1,32,256]{5,4,3,2,1,0:T(8,128)S(1)}, f32[1,3,2,1,32,256]{5,4,3,2,1,0:T(8,128)S(1)}, u32[]{:S(2)}, u32[]{:S(2)}) collective-permute-start(f32[1,3,2,1,32,256]{5,4,3,2,1,0:T(8,128)S(1)} %slice.2170), channel_id=1, source_target_pairs={{2,0},{4,2},{6,4},{8,6},{10,8},{12,10},{14,12},{3,1},{5,3},{7,5},{... | collective-permute-start | bytes 589832 | tf_op jit(solution)/shard_map/ppermute | solution.py:15
  187.2 3.1 collective-permute-start.9
  195.6 4.9 collective-permute-start.11
  197.1 2.1 collective-permute-start.10
  247.1 7.8 %collective-permute-start.12 = (f32[1,3,2,1,32,256]{5,4,3,2,1,0:T(8,128)S(1)}, f32[1,3,2,1,32,256]{5,4,3,2,1,0:T(8,128)S(1)}, u32[]{:S(2)}, u32[]{:S(2)}) collective-permute-start(f32[1,3,2,1,32,256]{5,4,3,2,1,0:T(8,128)S(1)} %slice.2211), channel_id=1, source_target_pairs={{2,0},{4,2},{6,4},{8,6},{10,8},{12,10},{14,12},{3,1},{5,3},{7,5},{... | collective-permute-start | bytes 589832 | tf_op jit(solution)/shard_map/ppermute | solution.py:15
  248.4 3.1 collective-permute-start.13
  256.5 5.6 %collective-permute-start.15 = (f32[1,3,2,1,32,256]{5,4,3,2,1,0:T(8,128)S(1)}, f32[1,3,2,1,32,256]{5,4,3,2,1,0:T(8,128)S(1)}, u32[]{:S(2)}, u32[]{:S(2)}) collective-permute-start(f32[1,3,2,1,32,256]{5,4,3,2,1,0:T(8,128)S(1)} %pad_maximum_fusion.27), channel_id=1, source_target_pairs={{0,2},{2,4},{4,6},{6,8},{8,10},{10,12},{12,14},{1,3},{3,5},{5,7},{... | collective-permute-start | bytes 589832 | tf_op jit(solution)/shard_map/ppermute | solution.py:15
  258.0 3.9 collective-permute-start.14
  345.0 8.1 %collective-permute-start.16 = (f32[1,3,2,1,32,256]{5,4,3,2,1,0:T(8,128)S(1)}, f32[1,3,2,1,32,256]{5,4,3,2,1,0:T(8,128)S(1)}, u32[]{:S(2)}, u32[]{:S(2)}) collective-permute-start(f32[1,3,2,1,32,256]{5,4,3,2,1,0:T(8,128)S(1)} %slice.2254), channel_id=1, source_target_pairs={{2,0},{4,2},{6,4},{8,6},{10,8},{12,10},{14,12},{3,1},{5,3},{7,5},{... | collective-permute-start | bytes 589832 | tf_op jit(solution)/shard_map/ppermute | solution.py:15
  346.4 3.1 collective-permute-start.17
  354.8 5.3 %collective-permute-start.19 = (f32[1,3,2,1,32,256]{5,4,3,2,1,0:T(8,128)S(1)}, f32[1,3,2,1,32,256]{5,4,3,2,1,0:T(8,128)S(1)}, u32[]{:S(2)}, u32[]{:S(2)}) collective-permute-start(f32[1,3,2,1,32,256]{5,4,3,2,1,0:T(8,128)S(1)} %pad_maximum_fusion.25), channel_id=1, source_target_pairs={{0,2},{2,4},{4,6},{6,8},{8,10},{10,12},{12,14},{1,3},{3,5},{5,7},{... | collective-permute-start | bytes 589832 | tf_op jit(solution)/shard_map/ppermute | solution.py:15
  356.3 2.1 collective-permute-start.18
  414.4 4.9 collective-permute-start.21
  415.7 9.5 %collective-permute-start.20 = (f32[1,3,2,1,32,256]{5,4,3,2,1,0:T(8,128)S(1)}, f32[1,3,2,1,32,256]{5,4,3,2,1,0:T(8,128)S(1)}, u32[]{:S(2)}, u32[]{:S(2)}) collective-permute-start(f32[1,3,2,1,32,256]{5,4,3,2,1,0:T(8,128)S(1)} %slice.2295), channel_id=1, source_target_pairs={{2,0},{4,2},{6,4},{8,6},{10,8},{12,10},{14,12},{3,1},{5,3},{7,5},{... | collective-permute-start | bytes 589832 | tf_op jit(solution)/shard_map/ppermute | solution.py:15
  426.9 6.1 %collective-permute-start.22 = (f32[1,3,2,4,1,256]{5,4,3,2,1,0:T(1,128)S(1)}, f32[1,3,2,4,1,256]{5,4,3,2,1,0:T(1,128)S(1)}, u32[]{:S(2)}, u32[]{:S(2)}) collective-permute-start(f32[1,3,2,4,1,256]{5,4,3,2,1,0:T(1,128)S(1)} %pad_maximum_fusion.35), channel_id=1, source_target_pairs={{0,1},{2,3},{4,5},{6,7},{8,9},{10,11},{12,13},{14,15},{16,17},{18,... | collective-permute-start | bytes 73736 | tf_op jit(solution)/shard_map/ppermute | solution.py:15
  428.9 5.3 %collective-permute-start.23 = (f32[1,3,2,1,32,256]{5,4,3,2,1,0:T(8,128)S(1)}, f32[1,3,2,1,32,256]{5,4,3,2,1,0:T(8,128)S(1)}, u32[]{:S(2)}, u32[]{:S(2)}) collective-permute-start(f32[1,3,2,1,32,256]{5,4,3,2,1,0:T(8,128)S(1)} %pad_maximum_fusion.23), channel_id=1, source_target_pairs={{0,2},{2,4},{4,6},{6,8},{8,10},{10,12},{12,14},{1,3},{3,5},{5,7},{... | collective-permute-start | bytes 589832 | tf_op jit(solution)/shard_map/ppermute | solution.py:15
  (86 other events, 2204.7 us)
